TPU v7x, 32 devices: a whole 2x2x4 slice. The times are simulated.
32 devices in a mesh: head: 4 (over z), outer: 2 (over core), inner: 4 (over y, x).
Axes of the slice: x: 2, y: 2, z: 4, core: 2. Of those that a mesh axis runs over, the one named last changes fastest.
Arguments:
- query: bfloat16 [4096, 8192], P(('outer', 'inner', 'head')), may hold values from -100 to 100
- keys: bfloat16 [4096, 1024], P(('outer', 'inner', 'head')), may hold values from -4.5 to 4.5
- values: bfloat16 [4096, 1024], P(('outer', 'inner', 'head')), may hold values from -6 to 6
- lengths: int32 [8], replicated, may hold values from 1 to 1024, 4096 in all
Outputs:
- attended: bfloat16 [4096, 8192], P(('outer', 'inner', 'head'))
Inputs may be any that keep to these rules, and one draw needn't show every extreme that they name: `lengths`: they sum to 4096, and the longest is exactly 1024.
All inputs are finite; a program needn't handle non-finite values.
Results may differ from a plain program's by a relative error of at most 0.0038.
Values may be sent and summed in bfloat16 or wider, within the bound.
A program may use at most 64 MiB of HBM per device.

v0:
```python
import math
import jax
import jax.numpy as jnp
from jax import lax
from jax.sharding import PartitionSpec as P

HEAD_SIZE = 128


def from_behind(value, axis, steps):
    count = lax.axis_size(axis)
    leading, last = (max(0, -steps), min(count, count - steps))
    return lax.ppermute(value, axis, [(source, source + steps) for source in range(leading, last)])


def doc_numbers(lengths, start_pos, count):
    ends = jnp.cumsum(lengths)
    positions = start_pos + lax.iota(jnp.int32, count)
    numbers = jnp.sum((positions[:, None] >= ends[None, :]).astype(jnp.int32), axis=1)
    return (numbers, positions)


def per_device(query, keys, values, lengths):
    query_local, keys_local, values_local = (
        lax.all_to_all(query, "head", split_axis=1, concat_axis=0, tiled=True),
        lax.all_to_all(keys, "head", split_axis=1, concat_axis=0, tiled=True),
        lax.all_to_all(values, "head", split_axis=1, concat_axis=0, tiled=True),
    )
    local_len = query_local.shape[0]
    pair_heads = keys_local.shape[1] // HEAD_SIZE
    group_width = query_local.shape[1] // keys_local.shape[1]
    context_count = lax.axis_size(("outer", "inner"))
    reach_hops = min(2, context_count // 4)
    position_index = lax.axis_index(("outer", "inner"))
    query_docs, query_pos = doc_numbers(lengths, position_index * local_len, local_len)
    query_groups = jnp.transpose(
        query_local.reshape(local_len, pair_heads, group_width, HEAD_SIZE), (2, 0, 1, 3)
    )
    score_scale = 1.0 / math.sqrt(HEAD_SIZE)

    def attend(state, stacked, distance):
        key_heads = stacked[0].reshape(local_len, pair_heads, HEAD_SIZE)
        value_heads = stacked[1].reshape(local_len, pair_heads, HEAD_SIZE)
        key_docs, key_pos = doc_numbers(lengths, (position_index - distance) * local_len, local_len)
        visible = (
            (query_docs[:, None] == key_docs[None, :])
            & (key_pos[None, :] <= query_pos[:, None])
            & (key_pos[None, :] >= 0)
        )

        def one_group(operands):
            query_part, running_max, running_total, running_sum = operands
            scores = (
                jnp.einsum(
                    "qkd,ckd->kqc", query_part, key_heads, preferred_element_type=jnp.float32
                )
                * score_scale
            )
            masked = jnp.where(visible, scores, -1e30)
            new_max = jnp.maximum(running_max, jnp.max(masked, axis=2))
            weights = jnp.where(visible, jnp.exp(masked - new_max[..., None]), 0.0)
            shrink = jnp.exp(running_max - new_max)
            new_total = running_total * shrink + jnp.sum(weights, axis=2)
            update = jnp.einsum(
                "kqc,ckd->qkd",
                weights.astype(jnp.bfloat16),
                value_heads,
                preferred_element_type=jnp.float32,
            )
            new_sum = running_sum * jnp.transpose(shrink, (1, 0))[..., None] + update
            return (new_max, new_total, new_sum)

        return lax.map(one_group, (query_groups, state[0], state[1], state[2]))

    start_state = (
        jnp.full((group_width, pair_heads, local_len), -1e30, jnp.float32),
        jnp.zeros((group_width, pair_heads, local_len), jnp.float32),
        jnp.zeros((group_width, local_len, pair_heads, HEAD_SIZE), jnp.float32),
    )
    own_pair = jnp.stack((keys_local, values_local))
    state = attend(start_state, own_pair, 0)
    carried = own_pair
    for distance in range(1, reach_hops + 1):
        carried = from_behind(carried, ("outer", "inner"), 1)
        state = attend(state, carried, distance)
    running_max, running_total, running_sum = state
    outcome = running_sum / jnp.transpose(running_total, (0, 2, 1))[..., None]
    outcome = jnp.transpose(outcome, (1, 2, 0, 3))
    outcome = outcome.reshape(local_len, pair_heads * group_width * HEAD_SIZE).astype(jnp.bfloat16)
    return lax.all_to_all(outcome, "head", split_axis=0, concat_axis=1, tiled=True)


def solution(mesh):
    placed = (
        P(("outer", "inner", "head"), None),
        P(("outer", "inner", "head"), None),
        P(("outer", "inner", "head"), None),
        P(),
    )
    return jax.shard_map(
        per_device,
        mesh=mesh,
        in_specs=placed,
        out_specs=P(("outer", "inner", "head"), None),
        check_vma=False,
    )
```

profile of v0, /device:TPU:0, one launch (start us, length us, event | category | flops | bytes accessed | tf_op | source)
XLA Modules:
  0.0 246.9 jit_solution(3934203246122695590)
XLA Ops:
  1.9 6.3 %all-to-all-start.1 = ((bf16[128,4,256]{0,2,1:T(8,128)(2,1)}), bf16[128,4,256]{0,2,1:T(8,128)(2,1)S(1)}, u32[]{:S(2)}, u32[]{:S(2)}) async-start(bf16[128,4,256]{0,2,1:T(8,128)(2,1)} %bitcast.2), calls=%async_computation.1 | async-start | bytes 524288 | tf_op jit(solution)/shard_map/all_to_all | solution.py:26
  10.1 7.1 %all-to-all-done.1 = bf16[128,4,256]{0,2,1:T(8,128)(2,1)S(1)} async-done(((bf16[128,4,256]{0,2,1:T(8,128)(2,1)}), bf16[128,4,256]{0,2,1:T(8,128)(2,1)S(1)}, u32[]{:S(2)}, u32[]{:S(2)}) %all-to-all-start.1) | async-done | bytes 262176 | tf_op jit(solution)/shard_map/all_to_all | solution.py:26
  17.2 3.4 %all-to-all-start.2 = ((bf16[128,4,256]{0,2,1:T(8,128)(2,1)}), bf16[128,4,256]{0,2,1:T(8,128)(2,1)S(1)}, u32[]{:S(2)}, u32[]{:S(2)}) async-start(bf16[128,4,256]{0,2,1:T(8,128)(2,1)} %bitcast.4), calls=%async_computation.2 | async-start | bytes 524288 | tf_op jit(solution)/shard_map/all_to_all | solution.py:27
  22.2 5.4 %all-to-all-done.2 = bf16[128,4,256]{0,2,1:T(8,128)(2,1)S(1)} async-done(((bf16[128,4,256]{0,2,1:T(8,128)(2,1)}), bf16[128,4,256]{0,2,1:T(8,128)(2,1)S(1)}, u32[]{:S(2)}, u32[]{:S(2)}) %all-to-all-start.2) | async-done | bytes 262176 | tf_op jit(solution)/shard_map/all_to_all | solution.py:27
  27.6 3.6 %all-to-all-start = ((bf16[128,4,2048]{2,0,1:T(8,128)(2,1)}), bf16[128,4,2048]{2,0,1:T(8,128)(2,1)S(1)}, u32[]{:S(2)}, u32[]{:S(2)}) async-start(bf16[128,4,2048]{2,0,1:T(8,128)(2,1)} %bitcast.143), calls=%async_computation | async-start | bytes 4194304 | tf_op jit(solution)/shard_map/all_to_all | solution.py:25
  31.6 4.2 %collective-permute-start = (bf16[2,512,256]{2,1,0:T(8,128)(2,1)S(1)}, bf16[2,512,256]{2,1,0:T(8,128)(2,1)}, u32[]{:S(2)}, u32[]{:S(2)}) collective-permute-start(bf16[2,512,256]{2,1,0:T(8,128)(2,1)S(1)} %pad_maximum_fusion), channel_id=1, source_target_pairs={{0,1},{1,2},{2,3},{3,4},{4,5},{5,6},{6,7},{8,9},{9,10},{10,11},{11... | collective-permute-start | bytes 1572872 | tf_op jit(solution)/shard_map/ppermute | solution.py:13
  35.8 7.3 %collective-permute-done = bf16[2,512,256]{2,1,0:T(8,128)(2,1)} collective-permute-done((bf16[2,512,256]{2,1,0:T(8,128)(2,1)S(1)}, bf16[2,512,256]{2,1,0:T(8,128)(2,1)}, u32[]{:S(2)}, u32[]{:S(2)}) %collective-permute-start) | collective-permute-done | bytes 524320 | tf_op jit(solution)/shard_map/ppermute | solution.py:13
  43.2 5.3 %collective-permute-start.1 = (bf16[2,512,256]{2,1,0:T(8,128)(2,1)}, bf16[2,512,256]{2,1,0:T(8,128)(2,1)}, u32[]{:S(2)}, u32[]{:S(2)}) collective-permute-start(bf16[2,512,256]{2,1,0:T(8,128)(2,1)} %collective-permute-done), channel_id=1, source_target_pairs={{0,1},{1,2},{2,3},{3,4},{4,5},{5,6},{6,7},{8,9},{9,10},{10,11},{11... | collective-permute-start | bytes 1572872 | tf_op jit(solution)/shard_map/ppermute | solution.py:13
  52.1 5.0 %collective-permute-done.1 = bf16[2,512,256]{2,1,0:T(8,128)(2,1)} collective-permute-done((bf16[2,512,256]{2,1,0:T(8,128)(2,1)}, bf16[2,512,256]{2,1,0:T(8,128)(2,1)}, u32[]{:S(2)}, u32[]{:S(2)}) %collective-permute-start.1) | collective-permute-done | bytes 524320 | tf_op jit(solution)/shard_map/ppermute | solution.py:13
  58.8 17.9 %all-to-all-done = bf16[128,4,2048]{2,0,1:T(8,128)(2,1)S(1)} async-done(((bf16[128,4,2048]{2,0,1:T(8,128)(2,1)}), bf16[128,4,2048]{2,0,1:T(8,128)(2,1)S(1)}, u32[]{:S(2)}, u32[]{:S(2)}) %all-to-all-start) | async-done | bytes 2097184 | tf_op jit(solution)/shard_map/all_to_all | solution.py:25
  80.3 27.0 %while.43 = (s32[]{:T(128)}, f32[8,2,512]{2,1,0:T(2,128)S(1)}, f32[8,2,512]{2,1,0:T(2,128)S(1)}, f32[8,512,2,128]{3,1,2,0:T(8,128)}, bf16[8,512,2,128]{3,1,2,0:T...) while((s32[]{:T(128)}, f32[8,2,512]{2,1,0:T(2,128)S(1)}, ...), condition=%wide.region_5.6_spmd.clone, body=%wide.region_2.0_spmd.clone.sunk | while | flops 276435968 | bytes 9753745 | solution.py:73
  109.6 34.8 %while.44 = (s32[]{:T(128)}, f32[8,2,512]{2,1,0:T(2,128)S(1)}, f32[8,2,512]{2,1,0:T(2,128)S(1)}, f32[8,512,2,128]{3,1,2,0:T(8,128)}, f32[8,2,512]{2,1,0:T(2,128)...) while((s32[]{:T(128)}, f32[8,2,512]{2,1,0:T(2,128)S(1)}, ...), condition=%wide.region_10.11_spmd.clone, body=%wide.region_7.10_spmd.clone.sunk | while | flops 276566016 | bytes 9245857 | solution.py:73
  114.9 2.8 %fusion.119 = f32[8,512,2,128]{3,1,2,0:T(8,128)} fusion(f32[8,512,2,128]{3,1,2,0:T(8,128)} %get-tuple-element.807, s32[]{:T(128)} %get-tuple-element.804, bf16[512,2,128]{2,0,1:T(8,128)(2,1)S(1)} %get-tuple-element.829, f32[2,512,512]{1,2,0:T(8,128)S(1)} %get-tuple-element.731, f32[2,512]{1,0:T(2,128)S(1)} %get-tuple-element.733, ...), kind=kOutput, calls=%fused_computation.40.clone.1 | convolution fusion | flops 137101312 | bytes 3678720 | tf_op jit(solution)/shard_map/while/body/eval_jaxpr/kqc,ckd->qkd/dot_general | solution.py:64
  119.2 2.8 %fusion.119 = f32[8,512,2,128]{3,1,2,0:T(8,128)} fusion(f32[8,512,2,128]{3,1,2,0:T(8,128)} %get-tuple-element.807, s32[]{:T(128)} %get-tuple-element.804, bf16[512,2,128]{2,0,1:T(8,128)(2,1)S(1)} %get-tuple-element.829, f32[2,512,512]{1,2,0:T(8,128)S(1)} %get-tuple-element.731, f32[2,512]{1,0:T(2,128)S(1)} %get-tuple-element.733, ...), kind=kOutput, calls=%fused_computation.40.clone.1 | convolution fusion | flops 137101312 | bytes 3678720 | tf_op jit(solution)/shard_map/while/body/eval_jaxpr/kqc,ckd->qkd/dot_general | solution.py:64
  123.6 2.8 %fusion.119 = f32[8,512,2,128]{3,1,2,0:T(8,128)} fusion(f32[8,512,2,128]{3,1,2,0:T(8,128)} %get-tuple-element.807, s32[]{:T(128)} %get-tuple-element.804, bf16[512,2,128]{2,0,1:T(8,128)(2,1)S(1)} %get-tuple-element.829, f32[2,512,512]{1,2,0:T(8,128)S(1)} %get-tuple-element.731, f32[2,512]{1,0:T(2,128)S(1)} %get-tuple-element.733, ...), kind=kOutput, calls=%fused_computation.40.clone.1 | convolution fusion | flops 137101312 | bytes 3678720 | tf_op jit(solution)/shard_map/while/body/eval_jaxpr/kqc,ckd->qkd/dot_general | solution.py:64
  132.3 2.8 %fusion.119 = f32[8,512,2,128]{3,1,2,0:T(8,128)} fusion(f32[8,512,2,128]{3,1,2,0:T(8,128)} %get-tuple-element.807, s32[]{:T(128)} %get-tuple-element.804, bf16[512,2,128]{2,0,1:T(8,128)(2,1)S(1)} %get-tuple-element.829, f32[2,512,512]{1,2,0:T(8,128)S(1)} %get-tuple-element.731, f32[2,512]{1,0:T(2,128)S(1)} %get-tuple-element.733, ...), kind=kOutput, calls=%fused_computation.40.clone.1 | convolution fusion | flops 137101312 | bytes 3678720 | tf_op jit(solution)/shard_map/while/body/eval_jaxpr/kqc,ckd->qkd/dot_general | solution.py:64
  141.0 2.8 %fusion.119 = f32[8,512,2,128]{3,1,2,0:T(8,128)} fusion(f32[8,512,2,128]{3,1,2,0:T(8,128)} %get-tuple-element.807, s32[]{:T(128)} %get-tuple-element.804, bf16[512,2,128]{2,0,1:T(8,128)(2,1)S(1)} %get-tuple-element.829, f32[2,512,512]{1,2,0:T(8,128)S(1)} %get-tuple-element.731, f32[2,512]{1,0:T(2,128)S(1)} %get-tuple-element.733, ...), kind=kOutput, calls=%fused_computation.40.clone.1 | convolution fusion | flops 137101312 | bytes 3678720 | tf_op jit(solution)/shard_map/while/body/eval_jaxpr/kqc,ckd->qkd/dot_general | solution.py:64
  146.8 34.8 %while.45 = (s32[]{:T(128)}, f32[8,2,512]{2,1,0:T(2,128)S(1)}, f32[8,512,2,128]{3,1,2,0:T(8,128)}, f32[8,2,512]{2,1,0:T(2,128)S(1)}, f32[8,2,512]{2,1,0:T(2,128)...) while((s32[]{:T(128)}, f32[8,2,512]{2,1,0:T(2,128)S(1)}, ...), condition=%wide.region_15.16_spmd.clone, body=%wide.region_12.15_spmd.clone.sunk | while | flops 276566016 | bytes 9241753 | solution.py:73
  152.1 2.8 %fusion.127 = f32[8,512,2,128]{3,1,2,0:T(8,128)} fusion(f32[8,512,2,128]{3,1,2,0:T(8,128)} %get-tuple-element.853, s32[]{:T(128)} %get-tuple-element.851, bf16[512,2,128]{2,0,1:T(8,128)(2,1)S(1)} %get-tuple-element.874, f32[2,512,512]{1,2,0:T(8,128)S(1)} %get-tuple-element.751, f32[2,512]{1,0:T(2,128)S(1)} %get-tuple-element.753, ...), kind=kOutput, calls=%fused_computation.71.clone.1 | convolution fusion | flops 137101312 | bytes 3678720 | tf_op jit(solution)/shard_map/while/body/eval_jaxpr/kqc,ckd->qkd/dot_general | solution.py:64
  169.5 2.9 %fusion.127 = f32[8,512,2,128]{3,1,2,0:T(8,128)} fusion(f32[8,512,2,128]{3,1,2,0:T(8,128)} %get-tuple-element.853, s32[]{:T(128)} %get-tuple-element.851, bf16[512,2,128]{2,0,1:T(8,128)(2,1)S(1)} %get-tuple-element.874, f32[2,512,512]{1,2,0:T(8,128)S(1)} %get-tuple-element.751, f32[2,512]{1,0:T(2,128)S(1)} %get-tuple-element.753, ...), kind=kOutput, calls=%fused_computation.71.clone.1 | convolution fusion | flops 137101312 | bytes 3678720 | tf_op jit(solution)/shard_map/while/body/eval_jaxpr/kqc,ckd->qkd/dot_general | solution.py:64
  181.6 2.9 %fusion.73 = bf16[512,2,8,128]{3,0,1,2:T(8,128)(2,1)S(1)} fusion(f32[8,512,2,128]{3,1,2,0:T(8,128)} %get-tuple-element.167, f32[8,512,2]{1,2,0:T(2,128)S(1)} %bitcast.213), kind=kLoop, calls=%fused_computation.96 | loop fusion | flops 2097152 | bytes 6324224 | tf_op jit(solution)/shard_map/convert_element_type | solution.py:89
  190.0 51.0 %all_to_all.64 = bf16[4,128,2048]{2,1,0:T(8,128)(2,1)} all-to-all(bf16[4,128,2048]{2,1,0:T(8,128)(2,1)S(1)} %convert_element_type.34), channel_id=1, replica_groups=mesh['head'=4,'outer'=2,'inner'=4] {'head'}, dimensions={0} | all-to-all | bytes 4194304 | tf_op jit(solution)/shard_map/all_to_all | solution.py:90
  241.0 3.0 %copy.76 = bf16[128,4,2048]{0,2,1:T(8,128)(2,1)S(1)} copy(bf16[128,4,2048]{2,0,1:T(8,128)(2,1)} %bitcast.202) | data formatting | bytes 4194304 | tf_op jit(solution)/shard_map/all_to_all | solution.py:90
  244.0 2.9 %copy.77 = bf16[128,8192]{1,0:T(8,128)(2,1)} copy(bf16[128,8192]{0,1:T(8,128)(2,1)S(1)} %bitcast.203) | data formatting | bytes 4194304 | tf_op jit(solution)/shard_map/all_to_all | solution.py:90
  (198 shorter events, 100.2 us)
Async XLA Ops:
  0.0 20.6 %copy-start = (bf16[128,8192]{1,0:T(8,128)(2,1)S(1)}, bf16[128,8192]{1,0:T(8,128)(2,1)}, u32[]{:S(2)}) copy-start(bf16[128,8192]{1,0:T(8,128)(2,1)} %param.10) | copy-start | bytes 6291460
  1.9 15.3 %all-to-all-start.1 = ((bf16[128,4,256]{0,2,1:T(8,128)(2,1)}), bf16[128,4,256]{0,2,1:T(8,128)(2,1)S(1)}, u32[]{:S(2)}, u32[]{:S(2)}) async-start(bf16[128,4,256]{0,2,1:T(8,128)(2,1)} %bitcast.2), calls=%async_computation.1 | async-start | bytes 524288 | tf_op jit(solution)/shard_map/all_to_all | solution.py:26
  17.2 10.4 %all-to-all-start.2 = ((bf16[128,4,256]{0,2,1:T(8,128)(2,1)}), bf16[128,4,256]{0,2,1:T(8,128)(2,1)S(1)}, u32[]{:S(2)}, u32[]{:S(2)}) async-start(bf16[128,4,256]{0,2,1:T(8,128)(2,1)} %bitcast.4), calls=%async_computation.2 | async-start | bytes 524288 | tf_op jit(solution)/shard_map/all_to_all | solution.py:27
  27.6 49.0 %all-to-all-start = ((bf16[128,4,2048]{2,0,1:T(8,128)(2,1)}), bf16[128,4,2048]{2,0,1:T(8,128)(2,1)S(1)}, u32[]{:S(2)}, u32[]{:S(2)}) async-start(bf16[128,4,2048]{2,0,1:T(8,128)(2,1)} %bitcast.143), calls=%async_computation | async-start | bytes 4194304 | tf_op jit(solution)/shard_map/all_to_all | solution.py:25
  31.2 17.2 %copy-start.3 = (s32[8]{0:T(128)S(1)}, s32[8]{0:T(128)}, u32[]{:S(2)}) copy-start(s32[8]{0:T(128)} %param.13) | copy-start | bytes 100
  31.6 11.6 %collective-permute-start = (bf16[2,512,256]{2,1,0:T(8,128)(2,1)S(1)}, bf16[2,512,256]{2,1,0:T(8,128)(2,1)}, u32[]{:S(2)}, u32[]{:S(2)}) collective-permute-start(bf16[2,512,256]{2,1,0:T(8,128)(2,1)S(1)} %pad_maximum_fusion), channel_id=1, source_target_pairs={{0,1},{1,2},{2,3},{3,4},{4,5},{5,6},{6,7},{8,9},{9,10},{10,11},{11... | collective-permute-start | bytes 1572872 | tf_op jit(solution)/shard_map/ppermute | solution.py:13
  43.2 13.9 %collective-permute-start.1 = (bf16[2,512,256]{2,1,0:T(8,128)(2,1)}, bf16[2,512,256]{2,1,0:T(8,128)(2,1)}, u32[]{:S(2)}, u32[]{:S(2)}) collective-permute-start(bf16[2,512,256]{2,1,0:T(8,128)(2,1)} %collective-permute-done), channel_id=1, source_target_pairs={{0,1},{1,2},{2,3},{3,4},{4,5},{5,6},{6,7},{8,9},{9,10},{10,11},{11... | collective-permute-start | bytes 1572872 | tf_op jit(solution)/shard_map/ppermute | solution.py:13
  80.5 1.0 copy-start.2
  83.8 1.0 copy-start.2
  87.2 1.0 copy-start.2
  90.5 1.0 copy-start.2
  93.9 1.0 copy-start.2
  97.2 1.0 copy-start.2
  100.6 1.0 copy-start.2
  103.9 1.0 copy-start.2
  107.2 2.4 copy-start.1
where the time goes:
time: 249 us; the launch traced here: 247 us
  matrix products  73 us (29%)
  blocking collectives  51 us (20%)
  waiting for transfers between devices  42.7 us (17%)
  local copies, waits for them, and re-layouts  30.7 us (12%)
  other arithmetic  25.2 us (10%)
  starting transfers between devices  22.9 us (9%)
    dot_general x24, matrix products, one_group(): jnp.einsum('kqc,ckd->qkd', weights.astype(jnp.bfloat16), value_heads, pre...  59.7 us
    all_to_all x1, blocking collectives, per_device(): lax.all_to_all(outcome, 'head', split_axis=0, concat_axis=1, tiled=True)  51 us
    all_to_all x1, waiting for transfers between devices, per_device(): lax.all_to_all(query, 'head', split_axis=1, concat_axis=0, tiled=True)  17.9 us
    reduce_sum x24, other arithmetic, one_group(): new_total = running_total * shrink + jnp.sum(weights, axis=2)  13.5 us
    dot_general x24, matrix products, one_group(): jnp.einsum('qkd,ckd->kqc', query_part, key_heads, preferred_element_type=...  13.3 us
    ppermute x2, waiting for transfers between devices, from_behind(): lax.ppermute(value, axis, [(source, source + steps) for source in range(l...  12.3 us
    ppermute x2, starting transfers between devices, from_behind(): lax.ppermute(value, axis, [(source, source + steps) for source in range(l...  9.49 us
    and x24, other arithmetic, attend(): (query_docs[:, None] == key_docs[None, :]) & (key_pos[None, :] <= query_p...  7.46 us
  transfers between devices with their start and end apart: 5, of which 5 were waited for; matrix products, arithmetic and copies ran while one was open for 4% of the time, Pallas kernels for 0%

commit v1 on v0

--- a/solution.py
+++ b/solution.py
@@ -1,3 +1,4 @@
+import functools
 import math
 import jax
 import jax.numpy as jnp
@@ -5,6 +6,21 @@
 from jax.sharding import PartitionSpec as P
 
 HEAD_SIZE = 128
+
+
+def plane_reach(inner_x, at_axis, d_out):
+    return jnp.concatenate(
+        jax.lax.all_to_all(
+            jnp.stack(jnp.split(inner_x, jax.lax.axis_size("head"), axis=at_axis), axis=0),
+            "head",
+            0,
+            0,
+        ),
+        d_out,
+    )
+
+
+turn_the_map = functools.partial(plane_reach, at_axis=1, d_out=0)
 
 
 def from_behind(value, axis, steps):
@@ -22,7 +38,7 @@
 
 def per_device(query, keys, values, lengths):
     query_local, keys_local, values_local = (
-        lax.all_to_all(query, "head", split_axis=1, concat_axis=0, tiled=True),
+        turn_the_map(query),
         lax.all_to_all(keys, "head", split_axis=1, concat_axis=0, tiled=True),
         lax.all_to_all(values, "head", split_axis=1, concat_axis=0, tiled=True),
     )

time: 249 us -> 248 us (level)
  local copies, waits for them, and re-layouts: 30.7 us -> 28.1 us
    another operation x8 -> x9, local copies, waits for them, and re-layouts: 7.23 us -> 7.37 us
where the time goes in v1:
time: 248 us; the launch traced here: 246 us
  matrix products  73 us (29%)
  blocking collectives  51.3 us (21%)
  waiting for transfers between devices  42.6 us (17%)
  local copies, waits for them, and re-layouts  28.1 us (11%)
  other arithmetic  26.8 us (11%)
  starting transfers between devices  22.9 us (9%)
    dot_general x24, matrix products, one_group(): jnp.einsum('kqc,ckd->qkd', weights.astype(jnp.bfloat16), value_heads, pre...  59.7 us
    all_to_all x1, blocking collectives, per_device(): lax.all_to_all(outcome, 'head', split_axis=0, concat_axis=1, tiled=True)  51.3 us
    all_to_all x1, waiting for transfers between devices, plane_reach(): jax.lax.all_to_all(jnp.stack(jnp.split(inner_x, jax.lax.axis_size('head')...  17.9 us
    reduce_sum x24, other arithmetic, one_group(): new_total = running_total * shrink + jnp.sum(weights, axis=2)  13.6 us
    dot_general x24, matrix products, one_group(): jnp.einsum('qkd,ckd->kqc', query_part, key_heads, preferred_element_type=...  13.3 us
    ppermute x2, waiting for transfers between devices, from_behind(): lax.ppermute(value, axis, [(source, source + steps) for source in range(l...  12.3 us
    ppermute x2, starting transfers between devices, from_behind(): lax.ppermute(value, axis, [(source, source + steps) for source in range(l...  9.49 us
    and x24, other arithmetic, attend(): (query_docs[:, None] == key_docs[None, :]) & (key_pos[None, :] <= query_p...  7.46 us
  transfers between devices with their start and end apart: 5, of which 5 were waited for; matrix products, arithmetic and copies ran while one was open for 4% of the time, Pallas kernels for 0%

profile of v1, /device:TPU:0, one launch (start us, length us, event | category | flops | bytes accessed | tf_op | source)
XLA Modules:
  0.0 246.1 jit_solution(13038006075677905374)
XLA Ops:
  1.9 6.3 %all-to-all-start.1 = ((bf16[128,4,256]{0,2,1:T(8,128)(2,1)}), bf16[128,4,256]{0,2,1:T(8,128)(2,1)S(1)}, u32[]{:S(2)}, u32[]{:S(2)}) async-start(bf16[128,4,256]{0,2,1:T(8,128)(2,1)} %bitcast.5), calls=%async_computation.1 | async-start | bytes 524288 | tf_op jit(solution)/shard_map/all_to_all | solution.py:42
  10.1 7.1 %all-to-all-done.1 = bf16[128,4,256]{0,2,1:T(8,128)(2,1)S(1)} async-done(((bf16[128,4,256]{0,2,1:T(8,128)(2,1)}), bf16[128,4,256]{0,2,1:T(8,128)(2,1)S(1)}, u32[]{:S(2)}, u32[]{:S(2)}) %all-to-all-start.1) | async-done | bytes 262176 | tf_op jit(solution)/shard_map/all_to_all | solution.py:42
  17.2 3.4 %all-to-all-start.2 = ((bf16[128,4,256]{0,2,1:T(8,128)(2,1)}), bf16[128,4,256]{0,2,1:T(8,128)(2,1)S(1)}, u32[]{:S(2)}, u32[]{:S(2)}) async-start(bf16[128,4,256]{0,2,1:T(8,128)(2,1)} %bitcast.7), calls=%async_computation.2 | async-start | bytes 524288 | tf_op jit(solution)/shard_map/all_to_all | solution.py:43
  22.4 5.3 %all-to-all-done.2 = bf16[128,4,256]{0,2,1:T(8,128)(2,1)S(1)} async-done(((bf16[128,4,256]{0,2,1:T(8,128)(2,1)}), bf16[128,4,256]{0,2,1:T(8,128)(2,1)S(1)}, u32[]{:S(2)}, u32[]{:S(2)}) %all-to-all-start.2) | async-done | bytes 262176 | tf_op jit(solution)/shard_map/all_to_all | solution.py:43
  27.6 3.6 %all-to-all-start = ((bf16[4,128,2048]{2,1,0:T(8,128)(2,1)}), bf16[4,128,2048]{2,1,0:T(8,128)(2,1)S(1)}, u32[]{:S(2)}, u32[]{:S(2)}) async-start(bf16[4,128,2048]{2,1,0:T(8,128)(2,1)} %pad_maximum_fusion), calls=%async_computation | async-start | bytes 4194304 | tf_op jit(solution)/shard_map/all_to_all | solution.py:13
  31.6 4.2 %collective-permute-start = (bf16[2,512,256]{2,1,0:T(8,128)(2,1)S(1)}, bf16[2,512,256]{2,1,0:T(8,128)(2,1)}, u32[]{:S(2)}, u32[]{:S(2)}) collective-permute-start(bf16[2,512,256]{2,1,0:T(8,128)(2,1)S(1)} %pad_maximum_fusion.1), channel_id=1, source_target_pairs={{0,1},{1,2},{2,3},{3,4},{4,5},{5,6},{6,7},{8,9},{9,10},{10,11},{11... | collective-permute-start | bytes 1572872 | tf_op jit(solution)/shard_map/ppermute | solution.py:29
  35.8 7.3 %collective-permute-done = bf16[2,512,256]{2,1,0:T(8,128)(2,1)} collective-permute-done((bf16[2,512,256]{2,1,0:T(8,128)(2,1)S(1)}, bf16[2,512,256]{2,1,0:T(8,128)(2,1)}, u32[]{:S(2)}, u32[]{:S(2)}) %collective-permute-start) | collective-permute-done | bytes 524320 | tf_op jit(solution)/shard_map/ppermute | solution.py:29
  43.2 5.3 %collective-permute-start.1 = (bf16[2,512,256]{2,1,0:T(8,128)(2,1)}, bf16[2,512,256]{2,1,0:T(8,128)(2,1)}, u32[]{:S(2)}, u32[]{:S(2)}) collective-permute-start(bf16[2,512,256]{2,1,0:T(8,128)(2,1)} %collective-permute-done), channel_id=1, source_target_pairs={{0,1},{1,2},{2,3},{3,4},{4,5},{5,6},{6,7},{8,9},{9,10},{10,11},{11... | collective-permute-start | bytes 1572872 | tf_op jit(solution)/shard_map/ppermute | solution.py:29
  52.1 5.0 %collective-permute-done.1 = bf16[2,512,256]{2,1,0:T(8,128)(2,1)} collective-permute-done((bf16[2,512,256]{2,1,0:T(8,128)(2,1)}, bf16[2,512,256]{2,1,0:T(8,128)(2,1)}, u32[]{:S(2)}, u32[]{:S(2)}) %collective-permute-start.1) | collective-permute-done | bytes 524320 | tf_op jit(solution)/shard_map/ppermute | solution.py:29
  58.8 17.9 %all-to-all-done = bf16[4,128,2048]{2,1,0:T(8,128)(2,1)S(1)} async-done(((bf16[4,128,2048]{2,1,0:T(8,128)(2,1)}), bf16[4,128,2048]{2,1,0:T(8,128)(2,1)S(1)}, u32[]{:S(2)}, u32[]{:S(2)}) %all-to-all-start) | async-done | bytes 2097184 | tf_op jit(solution)/shard_map/all_to_all | solution.py:13
  80.3 27.0 %while.43 = (s32[]{:T(128)}, f32[8,2,512]{2,1,0:T(2,128)S(1)}, f32[8,2,512]{2,1,0:T(2,128)S(1)}, f32[8,512,2,128]{3,1,2,0:T(8,128)}, bf16[8,512,2,128]{3,1,2,0:T...) while((s32[]{:T(128)}, f32[8,2,512]{2,1,0:T(2,128)S(1)}, ...), condition=%wide.region_5.6_spmd.clone, body=%wide.region_2.0_spmd.clone.sunk | while | flops 276435968 | bytes 9753745 | solution.py:89
  109.6 34.8 %while.44 = (s32[]{:T(128)}, f32[8,2,512]{2,1,0:T(2,128)S(1)}, f32[8,2,512]{2,1,0:T(2,128)S(1)}, f32[8,512,2,128]{3,1,2,0:T(8,128)}, f32[8,2,512]{2,1,0:T(2,128)...) while((s32[]{:T(128)}, f32[8,2,512]{2,1,0:T(2,128)S(1)}, ...), condition=%wide.region_10.11_spmd.clone, body=%wide.region_7.10_spmd.clone.sunk | while | flops 276566016 | bytes 9245857 | solution.py:89
  119.2 2.8 %fusion.119 = f32[8,512,2,128]{3,1,2,0:T(8,128)} fusion(f32[8,512,2,128]{3,1,2,0:T(8,128)} %get-tuple-element.811, s32[]{:T(128)} %get-tuple-element.808, bf16[512,2,128]{2,0,1:T(8,128)(2,1)S(1)} %get-tuple-element.833, f32[2,512,512]{1,2,0:T(8,128)S(1)} %get-tuple-element.735, f32[2,512]{1,0:T(2,128)S(1)} %get-tuple-element.737, ...), kind=kOutput, calls=%fused_computation.40.clone.1 | convolution fusion | flops 137101312 | bytes 3678720 | tf_op jit(solution)/shard_map/while/body/eval_jaxpr/kqc,ckd->qkd/dot_general | solution.py:80
  123.6 2.8 %fusion.119 = f32[8,512,2,128]{3,1,2,0:T(8,128)} fusion(f32[8,512,2,128]{3,1,2,0:T(8,128)} %get-tuple-element.811, s32[]{:T(128)} %get-tuple-element.808, bf16[512,2,128]{2,0,1:T(8,128)(2,1)S(1)} %get-tuple-element.833, f32[2,512,512]{1,2,0:T(8,128)S(1)} %get-tuple-element.735, f32[2,512]{1,0:T(2,128)S(1)} %get-tuple-element.737, ...), kind=kOutput, calls=%fused_computation.40.clone.1 | convolution fusion | flops 137101312 | bytes 3678720 | tf_op jit(solution)/shard_map/while/body/eval_jaxpr/kqc,ckd->qkd/dot_general | solution.py:80
  132.3 2.8 %fusion.119 = f32[8,512,2,128]{3,1,2,0:T(8,128)} fusion(f32[8,512,2,128]{3,1,2,0:T(8,128)} %get-tuple-element.811, s32[]{:T(128)} %get-tuple-element.808, bf16[512,2,128]{2,0,1:T(8,128)(2,1)S(1)} %get-tuple-element.833, f32[2,512,512]{1,2,0:T(8,128)S(1)} %get-tuple-element.735, f32[2,512]{1,0:T(2,128)S(1)} %get-tuple-element.737, ...), kind=kOutput, calls=%fused_computation.40.clone.1 | convolution fusion | flops 137101312 | bytes 3678720 | tf_op jit(solution)/shard_map/while/body/eval_jaxpr/kqc,ckd->qkd/dot_general | solution.py:80
  141.0 2.8 %fusion.119 = f32[8,512,2,128]{3,1,2,0:T(8,128)} fusion(f32[8,512,2,128]{3,1,2,0:T(8,128)} %get-tuple-element.811, s32[]{:T(128)} %get-tuple-element.808, bf16[512,2,128]{2,0,1:T(8,128)(2,1)S(1)} %get-tuple-element.833, f32[2,512,512]{1,2,0:T(8,128)S(1)} %get-tuple-element.735, f32[2,512]{1,0:T(2,128)S(1)} %get-tuple-element.737, ...), kind=kOutput, calls=%fused_computation.40.clone.1 | convolution fusion | flops 137101312 | bytes 3678720 | tf_op jit(solution)/shard_map/while/body/eval_jaxpr/kqc,ckd->qkd/dot_general | solution.py:80
  146.8 34.8 %while.45 = (s32[]{:T(128)}, f32[8,2,512]{2,1,0:T(2,128)S(1)}, f32[8,512,2,128]{3,1,2,0:T(8,128)}, f32[8,2,512]{2,1,0:T(2,128)S(1)}, f32[8,2,512]{2,1,0:T(2,128)...) while((s32[]{:T(128)}, f32[8,2,512]{2,1,0:T(2,128)S(1)}, ...), condition=%wide.region_15.16_spmd.clone, body=%wide.region_12.15_spmd.clone.sunk | while | flops 276566016 | bytes 9241753 | solution.py:89
  152.1 2.9 %fusion.127 = f32[8,512,2,128]{3,1,2,0:T(8,128)} fusion(f32[8,512,2,128]{3,1,2,0:T(8,128)} %get-tuple-element.857, s32[]{:T(128)} %get-tuple-element.855, bf16[512,2,128]{2,0,1:T(8,128)(2,1)S(1)} %get-tuple-element.878, f32[2,512,512]{1,2,0:T(8,128)S(1)} %get-tuple-element.755, f32[2,512]{1,0:T(2,128)S(1)} %get-tuple-element.757, ...), kind=kOutput, calls=%fused_computation.71.clone.1 | convolution fusion | flops 137101312 | bytes 3678720 | tf_op jit(solution)/shard_map/while/body/eval_jaxpr/kqc,ckd->qkd/dot_general | solution.py:80
  160.8 2.8 %fusion.127 = f32[8,512,2,128]{3,1,2,0:T(8,128)} fusion(f32[8,512,2,128]{3,1,2,0:T(8,128)} %get-tuple-element.857, s32[]{:T(128)} %get-tuple-element.855, bf16[512,2,128]{2,0,1:T(8,128)(2,1)S(1)} %get-tuple-element.878, f32[2,512,512]{1,2,0:T(8,128)S(1)} %get-tuple-element.755, f32[2,512]{1,0:T(2,128)S(1)} %get-tuple-element.757, ...), kind=kOutput, calls=%fused_computation.71.clone.1 | convolution fusion | flops 137101312 | bytes 3678720 | tf_op jit(solution)/shard_map/while/body/eval_jaxpr/kqc,ckd->qkd/dot_general | solution.py:80
  169.5 2.9 %fusion.127 = f32[8,512,2,128]{3,1,2,0:T(8,128)} fusion(f32[8,512,2,128]{3,1,2,0:T(8,128)} %get-tuple-element.857, s32[]{:T(128)} %get-tuple-element.855, bf16[512,2,128]{2,0,1:T(8,128)(2,1)S(1)} %get-tuple-element.878, f32[2,512,512]{1,2,0:T(8,128)S(1)} %get-tuple-element.755, f32[2,512]{1,0:T(2,128)S(1)} %get-tuple-element.757, ...), kind=kOutput, calls=%fused_computation.71.clone.1 | convolution fusion | flops 137101312 | bytes 3678720 | tf_op jit(solution)/shard_map/while/body/eval_jaxpr/kqc,ckd->qkd/dot_general | solution.py:80
  178.2 2.8 %fusion.127 = f32[8,512,2,128]{3,1,2,0:T(8,128)} fusion(f32[8,512,2,128]{3,1,2,0:T(8,128)} %get-tuple-element.857, s32[]{:T(128)} %get-tuple-element.855, bf16[512,2,128]{2,0,1:T(8,128)(2,1)S(1)} %get-tuple-element.878, f32[2,512,512]{1,2,0:T(8,128)S(1)} %get-tuple-element.755, f32[2,512]{1,0:T(2,128)S(1)} %get-tuple-element.757, ...), kind=kOutput, calls=%fused_computation.71.clone.1 | convolution fusion | flops 137101312 | bytes 3678720 | tf_op jit(solution)/shard_map/while/body/eval_jaxpr/kqc,ckd->qkd/dot_general | solution.py:80
  181.6 2.9 %fusion.73 = bf16[512,2,8,128]{3,0,1,2:T(8,128)(2,1)S(1)} fusion(f32[8,512,2,128]{3,1,2,0:T(8,128)} %get-tuple-element.167, f32[8,512,2]{1,2,0:T(2,128)S(1)} %bitcast.215), kind=kLoop, calls=%fused_computation.96 | loop fusion | flops 2097152 | bytes 6324224 | tf_op jit(solution)/shard_map/convert_element_type | solution.py:105
  188.1 51.3 %all_to_all.53 = bf16[4,128,2048]{2,1,0:T(8,128)(2,1)S(1)} all-to-all(bf16[4,128,2048]{2,1,0:T(8,128)(2,1)} %convert_element_type.34), channel_id=1, replica_groups=mesh['head'=4,'outer'=2,'inner'=4] {'head'}, dimensions={0} | all-to-all | bytes 4194304 | tf_op jit(solution)/shard_map/all_to_all | solution.py:106
  242.0 4.1 %copy.74 = bf16[128,8192]{1,0:T(8,128)(2,1)} copy(bf16[128,8192]{0,1:T(8,128)(2,1)} %bitcast.206) | data formatting | bytes 4194304 | tf_op jit(solution)/shard_map/all_to_all | solution.py:106
  (199 shorter events, 98.2 us)
Async XLA Ops:
  0.0 20.6 %copy-start = (bf16[128,8192]{1,0:T(8,128)(2,1)S(1)}, bf16[128,8192]{1,0:T(8,128)(2,1)}, u32[]{:S(2)}) copy-start(bf16[128,8192]{1,0:T(8,128)(2,1)} %param.10) | copy-start | bytes 6291460
  1.9 15.3 %all-to-all-start.1 = ((bf16[128,4,256]{0,2,1:T(8,128)(2,1)}), bf16[128,4,256]{0,2,1:T(8,128)(2,1)S(1)}, u32[]{:S(2)}, u32[]{:S(2)}) async-start(bf16[128,4,256]{0,2,1:T(8,128)(2,1)} %bitcast.5), calls=%async_computation.1 | async-start | bytes 524288 | tf_op jit(solution)/shard_map/all_to_all | solution.py:42
  17.2 10.4 %all-to-all-start.2 = ((bf16[128,4,256]{0,2,1:T(8,128)(2,1)}), bf16[128,4,256]{0,2,1:T(8,128)(2,1)S(1)}, u32[]{:S(2)}, u32[]{:S(2)}) async-start(bf16[128,4,256]{0,2,1:T(8,128)(2,1)} %bitcast.7), calls=%async_computation.2 | async-start | bytes 524288 | tf_op jit(solution)/shard_map/all_to_all | solution.py:43
  27.6 49.0 %all-to-all-start = ((bf16[4,128,2048]{2,1,0:T(8,128)(2,1)}), bf16[4,128,2048]{2,1,0:T(8,128)(2,1)S(1)}, u32[]{:S(2)}, u32[]{:S(2)}) async-start(bf16[4,128,2048]{2,1,0:T(8,128)(2,1)} %pad_maximum_fusion), calls=%async_computation | async-start | bytes 4194304 | tf_op jit(solution)/shard_map/all_to_all | solution.py:13
  31.2 17.2 %copy-start.3 = (s32[8]{0:T(128)S(1)}, s32[8]{0:T(128)}, u32[]{:S(2)}) copy-start(s32[8]{0:T(128)} %param.13) | copy-start | bytes 100
  31.6 11.6 %collective-permute-start = (bf16[2,512,256]{2,1,0:T(8,128)(2,1)S(1)}, bf16[2,512,256]{2,1,0:T(8,128)(2,1)}, u32[]{:S(2)}, u32[]{:S(2)}) collective-permute-start(bf16[2,512,256]{2,1,0:T(8,128)(2,1)S(1)} %pad_maximum_fusion.1), channel_id=1, source_target_pairs={{0,1},{1,2},{2,3},{3,4},{4,5},{5,6},{6,7},{8,9},{9,10},{10,11},{11... | collective-permute-start | bytes 1572872 | tf_op jit(solution)/shard_map/ppermute | solution.py:29
  43.2 13.9 %collective-permute-start.1 = (bf16[2,512,256]{2,1,0:T(8,128)(2,1)}, bf16[2,512,256]{2,1,0:T(8,128)(2,1)}, u32[]{:S(2)}, u32[]{:S(2)}) collective-permute-start(bf16[2,512,256]{2,1,0:T(8,128)(2,1)} %collective-permute-done), channel_id=1, source_target_pairs={{0,1},{1,2},{2,3},{3,4},{4,5},{5,6},{6,7},{8,9},{9,10},{10,11},{11... | collective-permute-start | bytes 1572872 | tf_op jit(solution)/shard_map/ppermute | solution.py:29
  80.5 1.0 copy-start.2
  83.8 1.0 copy-start.2
  87.2 1.0 copy-start.2
  90.5 1.0 copy-start.2
  93.9 1.0 copy-start.2
  97.2 1.0 copy-start.2
  100.6 1.0 copy-start.2
  103.9 1.0 copy-start.2
  107.2 2.4 copy-start.1
